TPU v7x, 32 devices: a whole 2x2x4 slice. The times are simulated.
32 devices in a mesh: group: 4 (over x, core), member: 8 (over z, y).
Axes of the slice: x: 2, y: 2, z: 4, core: 2. Of those that a mesh axis runs over, the one named last changes fastest.
Arguments:
- embedded: bfloat16 [4096, 2048], P(('group', 'member')), may hold values from -6 to 6
- seq_lengths: int32 [32, 4], P(('group', 'member')), may hold values from 1 to 31, as said below
- client_gain: float32 [2048], replicated, may hold values from 0.1 to 1.9
- adapter_down: bfloat16 [2048, 128], P('member'), may hold values from -0.125 to 0.125
- adapter_up: bfloat16 [128, 2048], P(None, 'member'), may hold values from -0.5 to 0.5
- server_gain: float32 [2048], replicated, may hold values from 0.1 to 1.9
- gate_weight: bfloat16 [2048, 4096], P(None, 'group'), may hold values from -0.125 to 0.125
- up_weight: bfloat16 [2048, 4096], P(None, 'group'), may hold values from -0.125 to 0.125
- hidden_grad: bfloat16 [8, 4, 64, 4096], P('member', None, None, 'group'), may hold values from -6 to 6
Outputs:
- input_grad: bfloat16 [4096, 2048], P(('group', 'member'))
- delta_down: float32 [2048, 128], P('member')
- delta_up: float32 [128, 2048], P(None, 'member')
Inputs may be any that keep to these rules, and one draw needn't show every extreme that they name: `seq_lengths`: the lengths of one client's sequences sum to at most 64, and some client's lengths sum to exactly 64.
All inputs are finite; a program needn't handle non-finite values.
Results may differ from a plain program's by a relative error of at most 0.025.
Values may be sent and summed in bfloat16 or wider, within the bound.
No kernel may reach another device: no remote copies, remote signals or barrier semaphores. Data moves between devices by JAX's collectives and lax.ppermute only.
A program may use at most 64 MiB of HBM per device.

v0:
```python
import math
import jax
import jax.numpy as jnp
from jax import lax
from jax.sharding import PartitionSpec as P


def normalize(values, gain_vec):
    values = values.astype(jnp.float32)
    inverse = lax.rsqrt(jnp.mean(values * values, axis=-1, keepdims=True) + 1e-05)
    return values * inverse * gain_vec


def selector(lengths_row, slot_count, capacity, bucket, seq_count):
    slot_ids = lax.iota(jnp.int32, slot_count)
    seq_of = slot_ids // bucket
    within = slot_ids % bucket
    matches = seq_of[:, None] == lax.iota(jnp.int32, seq_count)[None, :]
    before = jnp.cumsum(lengths_row) - lengths_row
    own_len = jnp.sum(jnp.where(matches, lengths_row[None, :], 0), axis=1)
    own_start = jnp.sum(jnp.where(matches, before[None, :], 0), axis=1)
    dest_row = own_start + within
    is_live = within < own_len
    chooser = (lax.iota(jnp.int32, capacity)[:, None] == dest_row[None, :]) & is_live[None, :]
    return chooser.astype(jnp.bfloat16)


def gated_grads(gate_value, up_value, upstream):
    sigmoid = jax.nn.sigmoid(gate_value)
    grad_gate = upstream * up_value * sigmoid * (1.0 + gate_value * (1.0 - sigmoid))
    grad_up = upstream * gate_value * sigmoid
    return (grad_gate.astype(jnp.bfloat16), grad_up.astype(jnp.bfloat16))


def body(
    embedded,
    seq_lengths,
    client_gain,
    adapter_down,
    adapter_up,
    server_gain,
    gate_weight,
    up_weight,
    hidden_grad,
):
    slot_count, model_width = embedded.shape
    seq_count = seq_lengths.shape[1]
    bucket = slot_count // seq_count
    capacity = slot_count // 2
    groups = lax.axis_size("group")
    members = lax.axis_size("member")
    full_down, full_up = (
        lax.all_gather(adapter_down, "member", axis=0, tiled=True),
        lax.all_gather(adapter_up, "member", axis=1, tiled=True),
    )
    normed = normalize(embedded, client_gain).astype(jnp.bfloat16)
    low_rank = jnp.dot(normed, full_down, preferred_element_type=jnp.float32).astype(jnp.bfloat16)
    cut_rows = (
        embedded.astype(jnp.float32)
        + jnp.dot(low_rank, full_up, preferred_element_type=jnp.float32)
    ).astype(jnp.bfloat16)
    chooser = selector(seq_lengths[0], slot_count, capacity, bucket, seq_count)
    packed = jnp.dot(chooser, cut_rows, preferred_element_type=jnp.float32).astype(jnp.bfloat16)
    outgoing = normalize(packed, server_gain).astype(jnp.bfloat16)
    arrived = lax.all_gather(outgoing, "group", axis=0, tiled=True)
    gate_value = jnp.dot(arrived, gate_weight, preferred_element_type=jnp.float32)
    up_value = jnp.dot(arrived, up_weight, preferred_element_type=jnp.float32)
    upstream = hidden_grad.reshape(groups * capacity, gate_weight.shape[1]).astype(jnp.float32)
    grad_gate, grad_up = gated_grads(gate_value, up_value, upstream)
    partial_sum = lax.dot_general(
        grad_gate, gate_weight, (((1,), (1,)), ((), ())), preferred_element_type=jnp.float32
    )
    partial_sum = partial_sum + lax.dot_general(
        grad_up, up_weight, (((1,), (1,)), ((), ())), preferred_element_type=jnp.float32
    )
    partial_sum = partial_sum.astype(jnp.bfloat16)
    returned = lax.all_to_all(
        partial_sum.reshape(groups, capacity, model_width),
        "group",
        split_axis=0,
        concat_axis=0,
        tiled=True,
    )
    d_server = jnp.sum(returned.astype(jnp.float32), axis=0)
    pullback = jax.vjp(lambda v: normalize(v, server_gain), packed.astype(jnp.float32))[1]
    d_packed = pullback(d_server)[0].astype(jnp.bfloat16)
    d_cut = lax.dot_general(
        chooser, d_packed, (((0,), (0,)), ((), ())), preferred_element_type=jnp.float32
    ).astype(jnp.bfloat16)
    up_term = lax.dot_general(
        low_rank, d_cut, (((0,), (0,)), ((), ())), preferred_element_type=jnp.float32
    )
    d_low = lax.dot_general(
        d_cut, full_up, (((1,), (1,)), ((), ())), preferred_element_type=jnp.float32
    ).astype(jnp.bfloat16)
    down_term = lax.dot_general(
        normed, d_low, (((0,), (0,)), ((), ())), preferred_element_type=jnp.float32
    )
    d_normed = lax.dot_general(
        d_low, full_down, (((1,), (1,)), ((), ())), preferred_element_type=jnp.float32
    )
    pull_client = jax.vjp(lambda v: normalize(v, client_gain), embedded.astype(jnp.float32))[1]
    input_grad = (d_cut.astype(jnp.float32) + pull_client(d_normed)[0]).astype(jnp.bfloat16)
    divisor = 8.0 * math.sqrt(float(groups * members))
    total_down, total_up = lax.psum((down_term, up_term), ("group", "member"))
    member = lax.axis_index("member")
    row_share = model_width // members
    share_down = lax.dynamic_slice_in_dim(total_down, member * row_share, row_share, 0)
    share_up = lax.dynamic_slice_in_dim(total_up, member * row_share, row_share, 1)
    return (input_grad, share_down / divisor, share_up / divisor)


def solution(mesh):
    in_specs = (
        P(("group", "member"), None),
        P(("group", "member"), None),
        P(),
        P("member", None),
        P(None, "member"),
        P(),
        P(None, "group"),
        P(None, "group"),
        P("member", None, None, "group"),
    )
    out_specs = (P(("group", "member"), None), P("member", None), P(None, "member"))
    return jax.shard_map(body, mesh=mesh, in_specs=in_specs, out_specs=out_specs, check_vma=False)
```

profile of v0, /device:TPU:0, one launch (start us, length us, event | category | flops | bytes accessed | tf_op | source)
XLA Modules:
  0.0 280.2 jit_solution(9537499042172422395)
XLA Ops:
  7.2 0.0 copy-start.1
  7.2 0.0 all-gather.2.cloned.1.call-start
  7.2 1.2 fusion.10
  8.5 33.2 %all_gather.9 = bf16[2048,128]{1,0:T(8,128)(2,1)S(1)} all-gather(bf16[256,128]{1,0:T(8,128)(2,1)} %param.12), channel_id=1, replica_groups=mesh['group'=4,'member'=8] {'member'}, dimensions={0}, use_global_device_ids=true | all-gather | bytes 589824 | tf_op jit(solution)/shard_map/all_gather | solution.py:53
  41.7 0.8 reduce-window_clone.1
  42.5 0.7 subtract_bitcast_fusion
  43.2 0.7 select_reduce_fusion
  44.0 31.5 %all_gather.10 = bf16[128,2048]{1,0:T(8,128)(2,1)S(1)} all-gather(bf16[128,256]{1,0:T(8,128)(2,1)} %param.13), channel_id=1, replica_groups=mesh['group'=4,'member'=8] {'member'}, dimensions={1}, use_global_device_ids=true | all-gather | bytes 589824 | tf_op jit(solution)/shard_map/all_gather | solution.py:54
  75.4 1.4 convolution_convert_fusion.3
  76.9 1.6 multiply_reduce_fusion.1
  78.5 0.0 copy-done.1
  78.5 0.0 copy-start.3
  78.5 0.8 multiply_convert_fusion
  79.3 0.0 all-gather.2.cloned.1.call-update
  79.3 0.0 all-reduce.3.cloned.1.call-start
  79.4 18.0 %all-gather.2.cloned.1.call-done = bf16[256,2048]{1,0:T(8,128)(2,1)} async-done(((bf16[64,2048]{1,0:T(8,128)(2,1)}), bf16[256,2048]{1,0:T(8,128)(2,1)}) %all-gather.2.cloned.1.call-update) | async-done | bytes 1048592 | tf_op jit(solution)/shard_map/all_gather | solution.py:65
  97.4 4.7 %fusion.39 = f32[256,1024]{1,0:T(8,128)} fusion(bf16[256,2048]{1,0:T(8,128)(2,1)} %all-gather.2.cloned.1.call-done, bf16[2048,1024]{1,0:T(8,128)(2,1)} %param.15), kind=kOutput, calls=%fused_computation.69 | convolution fusion | flops 1073741824 | bytes 6291456 | tf_op jit(solution)/shard_map/dot_general | solution.py:66
  102.1 0.0 copy-done.3
  102.1 8.0 %fusion.14 = f32[256,2048]{1,0:T(8,128)} fusion(bf16[2048,1024]{1,0:T(8,128)(2,1)} %param.15, bf16[256,2048]{1,0:T(8,128)(2,1)} %all-gather.2.cloned.1.call-done, bf16[2048,1024]{1,0:T(8,128)(2,1)} %param.16, bf16[256,1024]{1,0:T(8,128)(2,1)S(1)} %bitcast.24, f32[256,1024]{1,0:T(8,128)} %fusion.39), kind=kOutput, calls=%fused_computation.31 | convolution fusion | flops 2150367232 | bytes 13107200 | tf_op jit(solution)/shard_map/dot_general | solution.py:70
  110.1 4.5 %fusion = bf16[256,2048]{1,0:T(8,128)(2,1)S(1)} fusion(f32[256,2048]{1,0:T(8,128)} %fusion.14, bf16[2048,1024]{1,0:T(8,128)(2,1)} %param.16, f32[256,1024]{1,0:T(8,128)} %fusion.39, bf16[256,1024]{1,0:T(8,128)(2,1)S(1)} %bitcast.25), kind=kOutput, calls=%fused_computation.1 | convolution fusion | flops 1076625408 | bytes 8912896 | tf_op jit(solution)/shard_map/dot_general | solution.py:73
  114.6 0.0 copy-start
  114.7 0.0 copy-start.2
  114.7 17.0 %all_to_all.5 = bf16[4,64,2048]{2,1,0:T(8,128)(2,1)S(1)} all-to-all(bf16[4,64,2048]{2,1,0:T(8,128)(2,1)S(1)} %bitcast.22), channel_id=1, replica_groups=mesh['group'=4,'member'=8] {'group'}, dimensions={0} | all-to-all | bytes 2097152 | tf_op jit(solution)/shard_map/all_to_all | solution.py:77
  131.7 0.2 convert_reduce_fusion
  131.8 0.2 multiply_reduce_fusion
  132.0 0.4 convolution_convert_fusion
  132.4 1.3 fusion.40
  133.7 0.3 convolution_convert_fusion.2
  134.0 0.0 copy-done
  134.0 0.0 copy-done.2
  134.0 1.4 fusion.23
  135.4 0.0 all-reduce.3.cloned.1.call-update
  135.4 0.4 fusion.13
  135.8 1.1 fusion.9
  137.0 133.2 %all-reduce.3.cloned.1.call-done = (f32[2048,128]{1,0:T(8,128)}, f32[128,2048]{1,0:T(8,128)}) async-done(((f32[2048,128]{1,0:T(8,128)}, f32[128,2048]{1,0:T(8,128)}), (f32[2048,128]{1,0:T(8,128)}, f32[128,2048]{1,0:T(8,128)})) %all-reduce.3.cloned.1.call-update) | async-done | bytes 2097168 | tf_op jit(solution)/shard_map/psum | solution.py:105
  270.2 1.6 dynamic-slice_multiply_fusion
  271.8 1.6 dynamic-slice_multiply_fusion.1
  (7 shorter events, 0.1 us)
Async XLA Ops:
  7.2 71.3 %copy-start.1 = (f32[2048]{0:T(1024)S(1)}, f32[2048]{0:T(1024)}, u32[]{:S(2)}) copy-start(f32[2048]{0:T(1024)} %param.14) | copy-start | bytes 24580
  7.2 90.2 %all-gather.2.cloned.1.call-start = ((), (), s32[]{:S(2)}) async-start(), calls=%async_computation.1 | async-start | bytes 1310720 | tf_op jit(solution)/shard_map/all_gather | solution.py:65
  78.5 23.7 %copy-start.3 = (bf16[1,4,64,1024]{3,2,1,0:T(8,128)(2,1)S(1)}, bf16[1,4,64,1024]{3,2,1,0:T(8,128)(2,1)}, u32[]{:S(2)}) copy-start(bf16[1,4,64,1024]{3,2,1,0:T(8,128)(2,1)} %param.17) | copy-start | bytes 1572868
  79.3 190.9 %all-reduce.3.cloned.1.call-start = ((), (), s32[]{:S(2)}) async-start(), calls=%async_computation.2 | async-start | bytes 4194304 | tf_op jit(solution)/shard_map/psum | solution.py:105
  114.6 19.4 %copy-start = (bf16[128,2048]{1,0:T(8,128)(2,1)S(1)}, bf16[128,2048]{1,0:T(8,128)(2,1)}, u32[]{:S(2)}) copy-start(bf16[128,2048]{1,0:T(8,128)(2,1)} %param.9) | copy-start | bytes 1572868
  114.7 19.4 %copy-start.2 = (f32[2048]{0:T(1024)S(1)}, f32[2048]{0:T(1024)}, u32[]{:S(2)}) copy-start(f32[2048]{0:T(1024)} %param.11) | copy-start | bytes 24580
Sparse Core Ops, SparseCore 0:
  79.5 17.8 all-gather.1
  135.6 134.6 all-reduce.2
where the time goes:
time: 281 us; the launch traced here: 280 us
  waiting for transfers between devices  151 us (54%)
  blocking collectives  81.7 us (29%)
  matrix products  24 us (9%)
  between operations  14.2 us (5%)
  other arithmetic  8.93 us (3%)
    psum x1, waiting for transfers between devices, body(): total_down, total_up = lax.psum((down_term, up_term), ('group', 'member'))  133 us
    all_gather x1, blocking collectives, body(): lax.all_gather(adapter_down, 'member', axis=0, tiled=True)  33.2 us
    all_gather x1, blocking collectives, body(): lax.all_gather(adapter_up, 'member', axis=1, tiled=True)  31.5 us
    all_gather x1, waiting for transfers between devices, body(): arrived = lax.all_gather(outgoing, 'group', axis=0, tiled=True)  18 us
    all_to_all x1, blocking collectives, body(): lax.all_to_all(partial_sum.reshape(groups, capacity, model_width), 'group...  17 us
    dot_general x1, matrix products, body(): lax.dot_general(grad_gate, gate_weight, (((1,), (1,)), ((), ())), preferr...  8.01 us
  transfers between devices with their start and end apart: 2, of which 2 were waited for; matrix products, arithmetic and copies ran while one was open for 1% of the time, Pallas kernels for 0%

commit v1 on v0

--- a/solution.py
+++ b/solution.py
@@ -102,7 +102,7 @@
     pull_client = jax.vjp(lambda v: normalize(v, client_gain), embedded.astype(jnp.float32))[1]
     input_grad = (d_cut.astype(jnp.float32) + pull_client(d_normed)[0]).astype(jnp.bfloat16)
     divisor = 8.0 * math.sqrt(float(groups * members))
-    total_down, total_up = lax.psum((down_term, up_term), ("group", "member"))
+    total_down, total_up = lax.psum(lax.psum((down_term, up_term), "member"), "group")
     member = lax.axis_index("member")
     row_share = model_width // members
     share_down = lax.dynamic_slice_in_dim(total_down, member * row_share, row_share, 0)

time: 281 us -> 301 us (1.071)
  waiting for transfers between devices: 151 us -> 172 us
    psum x1 -> x2, waiting for transfers between devices: 133 us -> 154 us  [the longest x1 102 us: body(): lax.psum((down_term, up_term), 'member')]
  transfers between devices with their start and end apart: 2 -> 3, of which waited for: 2 -> 3; matrix products, arithmetic and copies ran while one was open for 1% -> 1% of each run, Pallas kernels for 0% -> 0%
where the time goes in v1:
time: 301 us
  waiting for transfers between devices  172 us (57%)
  blocking collectives  81.7 us (27%)
  matrix products  23.9 us (8%)
  between operations  13.9 us (5%)
  other arithmetic  8.95 us (3%)
    psum x1, waiting for transfers between devices, body(): lax.psum((down_term, up_term), 'member')  102 us
    psum x1, waiting for transfers between devices, body(): lax.psum(lax.psum((down_term, up_term), 'member'), 'group')  51.6 us
    all_gather x1, blocking collectives, body(): lax.all_gather(adapter_down, 'member', axis=0, tiled=True)  33.2 us
    all_gather x1, blocking collectives, body(): lax.all_gather(adapter_up, 'member', axis=1, tiled=True)  31.5 us
    all_gather x1, waiting for transfers between devices, body(): arrived = lax.all_gather(outgoing, 'group', axis=0, tiled=True)  18 us
    all_to_all x1, blocking collectives, body(): lax.all_to_all(partial_sum.reshape(groups, capacity, model_width), 'group...  17 us
    dot_general x1, matrix products, body(): lax.dot_general(grad_gate, gate_weight, (((1,), (1,)), ((), ())), preferr...  7.75 us
  transfers between devices with their start and end apart: 3, of which 3 were waited for; matrix products, arithmetic and copies ran while one was open for 1% of the time, Pallas kernels for 0%

profile of v1, /device:TPU:0, one launch (start us, length us, event | category | flops | bytes accessed | tf_op | source)
XLA Modules:
  0.0 300.6 jit_solution(3328908516440311171)
XLA Ops:
  7.2 0.0 copy-start.1
  7.2 0.0 all-gather.2.cloned.1.call-start
  7.2 1.2 fusion.10
  8.5 33.2 %all_gather.9 = bf16[2048,128]{1,0:T(8,128)(2,1)S(1)} all-gather(bf16[256,128]{1,0:T(8,128)(2,1)} %param.12), channel_id=1, replica_groups=mesh['group'=4,'member'=8] {'member'}, dimensions={0}, use_global_device_ids=true | all-gather | bytes 589824 | tf_op jit(solution)/shard_map/all_gather | solution.py:53
  41.7 0.8 reduce-window_clone.1
  42.5 0.7 subtract_bitcast_fusion
  43.2 0.7 select_reduce_fusion
  44.0 31.5 %all_gather.10 = bf16[128,2048]{1,0:T(8,128)(2,1)S(1)} all-gather(bf16[128,256]{1,0:T(8,128)(2,1)} %param.13), channel_id=1, replica_groups=mesh['group'=4,'member'=8] {'member'}, dimensions={1}, use_global_device_ids=true | all-gather | bytes 589824 | tf_op jit(solution)/shard_map/all_gather | solution.py:54
  75.4 1.4 convolution_convert_fusion.3
  76.9 1.6 multiply_reduce_fusion.1
  78.5 0.0 copy-done.1
  78.5 0.0 copy-start.4
  78.5 0.8 multiply_convert_fusion
  79.3 0.0 all-gather.2.cloned.1.call-update
  79.3 0.0 all-reduce.5.cloned.1.call-start
  79.4 18.0 %all-gather.2.cloned.1.call-done = bf16[256,2048]{1,0:T(8,128)(2,1)} async-done(((bf16[64,2048]{1,0:T(8,128)(2,1)}), bf16[256,2048]{1,0:T(8,128)(2,1)}) %all-gather.2.cloned.1.call-update) | async-done | bytes 1048592 | tf_op jit(solution)/shard_map/all_gather | solution.py:65
  97.4 0.0 copy-start.3
  97.4 4.8 %fusion.39 = f32[256,1024]{1,0:T(8,128)} fusion(bf16[256,2048]{1,0:T(8,128)(2,1)} %all-gather.2.cloned.1.call-done, bf16[2048,1024]{1,0:T(8,128)(2,1)} %param.15), kind=kOutput, calls=%fused_computation.69 | convolution fusion | flops 1073741824 | bytes 6291456 | tf_op jit(solution)/shard_map/dot_general | solution.py:66
  102.2 0.0 copy-done.4
  102.2 0.0 copy-done.3
  102.2 7.8 %fusion.14 = f32[256,2048]{1,0:T(8,128)} fusion(bf16[2048,1024]{1,0:T(8,128)(2,1)} %param.15, bf16[256,2048]{1,0:T(8,128)(2,1)S(1)} %copy-done.3, bf16[2048,1024]{1,0:T(8,128)(2,1)} %param.16, bf16[256,1024]{1,0:T(8,128)(2,1)S(1)} %bitcast.24, f32[256,1024]{1,0:T(8,128)} %fusion.39), kind=kOutput, calls=%fused_computation.31 | convolution fusion | flops 2150367232 | bytes 13107200 | tf_op jit(solution)/shard_map/dot_general | solution.py:70
  110.0 4.5 %fusion = bf16[256,2048]{1,0:T(8,128)(2,1)S(1)} fusion(f32[256,2048]{1,0:T(8,128)} %fusion.14, bf16[2048,1024]{1,0:T(8,128)(2,1)} %param.16, f32[256,1024]{1,0:T(8,128)} %fusion.39, bf16[256,1024]{1,0:T(8,128)(2,1)S(1)} %bitcast.25), kind=kOutput, calls=%fused_computation.1 | convolution fusion | flops 1076625408 | bytes 8912896 | tf_op jit(solution)/shard_map/dot_general | solution.py:73
  114.5 0.0 copy-start
  114.5 0.0 copy-start.2
  114.5 17.0 %all_to_all.5 = bf16[4,64,2048]{2,1,0:T(8,128)(2,1)S(1)} all-to-all(bf16[4,64,2048]{2,1,0:T(8,128)(2,1)S(1)} %bitcast.22), channel_id=1, replica_groups=mesh['group'=4,'member'=8] {'group'}, dimensions={0} | all-to-all | bytes 2097152 | tf_op jit(solution)/shard_map/all_to_all | solution.py:77
  131.5 0.2 convert_reduce_fusion
  131.6 0.2 multiply_reduce_fusion
  131.8 0.4 convolution_convert_fusion
  132.2 1.3 fusion.40
  133.5 0.3 convolution_convert_fusion.2
  133.9 0.0 copy-done
  133.9 0.0 copy-done.2
  133.9 1.4 fusion.23
  135.3 0.0 all-reduce.5.cloned.1.call-update
  135.3 0.0 all-reduce.7.cloned.1.call-start
  135.3 102.4 %all-reduce.5.cloned.1.call-done = (f32[2048,128]{1,0:T(8,128)}, f32[128,2048]{1,0:T(8,128)}) async-done(((f32[2048,128]{1,0:T(8,128)}, f32[128,2048]{1,0:T(8,128)}), (f32[2048,128]{1,0:T(8,128)}, f32[128,2048]{1,0:T(8,128)})) %all-reduce.5.cloned.1.call-update) | async-done | bytes 2097168 | tf_op jit(solution)/shard_map/psum | solution.py:105
  237.8 0.0 all-reduce.7.cloned.1.call-update
  237.8 0.4 fusion.13
  238.2 1.1 fusion.9
  239.4 51.6 %all-reduce.7.cloned.1.call-done = (f32[2048,128]{1,0:T(8,128)}, f32[128,2048]{1,0:T(8,128)}) async-done(((f32[2048,128]{1,0:T(8,128)}, f32[128,2048]{1,0:T(8,128)}), (f32[2048,128]{1,0:T(8,128)}, f32[128,2048]{1,0:T(8,128)})) %all-reduce.7.cloned.1.call-update) | async-done | bytes 2097168 | tf_op jit(solution)/shard_map/psum | solution.py:105
  291.0 1.6 dynamic-slice_multiply_fusion
  292.5 1.6 dynamic-slice_multiply_fusion.1
  (7 shorter events, 0.1 us)
Async XLA Ops:
  7.2 71.3 %copy-start.1 = (f32[2048]{0:T(1024)S(1)}, f32[2048]{0:T(1024)}, u32[]{:S(2)}) copy-start(f32[2048]{0:T(1024)} %param.14) | copy-start | bytes 24580
  7.2 90.2 %all-gather.2.cloned.1.call-start = ((), (), s32[]{:S(2)}) async-start(), calls=%async_computation.1 | async-start | bytes 1310720 | tf_op jit(solution)/shard_map/all_gather | solution.py:65
  78.5 23.7 %copy-start.4 = (bf16[1,4,64,1024]{3,2,1,0:T(8,128)(2,1)S(1)}, bf16[1,4,64,1024]{3,2,1,0:T(8,128)(2,1)}, u32[]{:S(2)}) copy-start(bf16[1,4,64,1024]{3,2,1,0:T(8,128)(2,1)} %param.17) | copy-start | bytes 1572868
  79.3 158.4 %all-reduce.5.cloned.1.call-start = ((), (), s32[]{:S(2)}) async-start(), calls=%async_computation.2 | async-start | bytes 4194304 | tf_op jit(solution)/shard_map/psum | solution.py:105
  97.4 4.8 %copy-start.3 = (bf16[256,2048]{1,0:T(8,128)(2,1)S(1)}, bf16[256,2048]{1,0:T(8,128)(2,1)}, u32[]{:S(2)}) copy-start(bf16[256,2048]{1,0:T(8,128)(2,1)} %all-gather.2.cloned.1.call-done) | copy-start | bytes 3145732
  114.5 19.4 %copy-start = (bf16[128,2048]{1,0:T(8,128)(2,1)S(1)}, bf16[128,2048]{1,0:T(8,128)(2,1)}, u32[]{:S(2)}) copy-start(bf16[128,2048]{1,0:T(8,128)(2,1)} %param.9) | copy-start | bytes 1572868
  114.5 19.4 %copy-start.2 = (f32[2048]{0:T(1024)S(1)}, f32[2048]{0:T(1024)}, u32[]{:S(2)}) copy-start(f32[2048]{0:T(1024)} %param.11) | copy-start | bytes 24580
  135.3 155.7 %all-reduce.7.cloned.1.call-start = ((), (), s32[]{:S(2)}) async-start(), calls=%async_computation.3 | async-start | bytes 4194304 | tf_op jit(solution)/shard_map/psum | solution.py:105
Sparse Core Ops, SparseCore 0:
  79.5 17.8 all-gather.1
  135.4 102.3 all-reduce.4
  240.2 50.6 all-reduce.6
